TPU v7x, 128 devices: a whole 4x4x4 slice. The times are simulated.
128 devices in a mesh: lat: 16 (over z, x), lon: 8 (over y, core).
Axes of the slice: x: 4, y: 4, z: 4, core: 2. Of those that a mesh axis runs over, the one named last changes fastest.
Arguments:
- grid_feat: bfloat16 [131072, 474], P(('lat', 'lon')), may hold values from -6 to 6
- grid_send: int32 [128, 4, 256], P(('lat', 'lon')), may hold values from 0 to 1023
- g2m_sender: int32 [524288], P(('lat', 'lon')), may hold values from 0 to 2047, as said below
- g2m_receiver: int32 [524288], P(('lat', 'lon')), may hold values from 0 to 320, as said below
- g2m_geom: float32 [4, 524288], P(None, ('lat', 'lon')), may hold values from -1 to 1
- mesh_geom: float32 [3, 40960], P(None, ('lat', 'lon')), may hold values from -1 to 1
- mesh_adjacent_lists: int32 [128, 8, 112], P(('lat', 'lon')), may hold values from 0 to 319
- mesh_far: int32 [128, 128, 4], P(('lat', 'lon')), may hold values from 0 to 319
- mesh_sender: int32 [524288], P(('lat', 'lon')), may hold values from 0 to 1727, as said below
- mesh_receiver: int32 [524288], P(('lat', 'lon')), may hold values from 0 to 320, as said below
- mesh_edge_geom: float32 [4, 524288], P(None, ('lat', 'lon')), may hold values from -1 to 1
- embed_in: bfloat16 [474, 512], replicated, may hold values from -0.25 to 0.25
- mesh_in: float32 [3, 512], replicated, may hold values from -3.5 to 3.5
- geo_in: float32 [3, 4, 512], replicated, may hold values from -3 to 3
- pair_in: bfloat16 [3, 4, 512, 512], replicated, may hold values from -0.1875 to 0.1875
- square_out: bfloat16 [8, 512, 512], replicated, may hold values from -0.25 to 0.25
Outputs:
- mesh_out: bfloat16 [40960, 512], P(('lat', 'lon'))
Inputs may be any that keep to these rules, and one draw needn't show every extreme that they name: grid_send[s, d, k] is a local grid row of device s, which it sends to the device that has s as its source for side offset o_d. `g2m_sender`: below 1024, a local grid row of the edge's device; else 1024 + d * 256 + k, a row of received_grid whose source exists. `g2m_receiver`: a local mesh row of the edge's device, or 320 for a padding edge; a device's live edges come first, and some device has all 4096 live. mesh_adjacent_lists[t, d, k] is a local mesh row of device t, which it sends to the device that has t as its source for neighbour offset n_d. mesh_far[t, q, k] is a local mesh row of device t, which it sends to device q. `mesh_sender`: below 320, a local mesh row of the edge's device; else a halo row of the edge's device, and a neighbour's row only where that neighbour exists. `mesh_receiver`: a local mesh row of the edge's device, or 320 for a padding edge; a device's live edges come first, and some device has all 4096 live.
All inputs are finite; a program needn't handle non-finite values.
Results may differ from a plain program's by a relative error of at most 0.015.
Values may be sent and summed in bfloat16 or wider, within the bound.
A program may use at most 128 MiB of HBM per device.

v0:
```python
import jax
import jax.numpy as jnp
from jax import lax
from jax.sharding import PartitionSpec as P

EPSILON = 1e-05
GRID_OFFSETS = ((-1, 0), (1, 0), (0, -1), (0, 1))


def from_behind(block, axis, distance):
    devices = range(lax.axis_size(axis))
    route = [(i - distance, i) for i in devices if i - distance in devices]
    return lax.ppermute(block, axis, route)


def from_behind_2(block, axis, distance):
    devices = range(lax.axis_size(axis))
    route = [((i - distance) % len(devices), i) for i in devices]
    return lax.ppermute(block, axis, route)


def layer_norm(values):
    centre = values - jnp.mean(values, axis=-1, keepdims=True)
    spread = jnp.mean(centre * centre, axis=-1, keepdims=True)
    return centre * lax.rsqrt(spread + EPSILON)


def two_layer(pre_act, out_weight):
    hidden = jax.nn.silu(pre_act).astype(jnp.bfloat16)
    return layer_norm(jnp.dot(hidden, out_weight, preferred_element_type=jnp.float32))


def edge_sums(sender_term, receiver_term, senders, receivers, geometry, geo_weight, out_weight):
    node_count = receiver_term.shape[0]
    row_ids = jnp.minimum(receivers, node_count - 1)
    pre_act = jnp.dot(geometry.T, geo_weight, precision=lax.Precision.HIGHEST)
    pre_act = pre_act + sender_term[senders] + receiver_term[row_ids]
    message = two_layer(pre_act, out_weight).astype(jnp.bfloat16)
    incidence = (receivers[None, :] == jnp.arange(node_count, dtype=jnp.int32)[:, None]).astype(
        jnp.bfloat16
    )
    return jnp.dot(incidence, message, preferred_element_type=jnp.float32)


def node_update(latent, edge_sum, section_weights, out_weight):
    pre_act = jnp.dot(latent, section_weights[2], preferred_element_type=jnp.float32)
    pre_act = pre_act + jnp.dot(
        edge_sum.astype(jnp.bfloat16), section_weights[3], preferred_element_type=jnp.float32
    )
    return (latent.astype(jnp.float32) + two_layer(pre_act, out_weight)).astype(jnp.bfloat16)


def per_device(
    grid_feat,
    grid_send,
    g2m_sender,
    g2m_receiver,
    g2m_geom,
    mesh_geom,
    mesh_adjacent_lists,
    mesh_far,
    mesh_sender,
    mesh_receiver,
    mesh_edge_geom,
    embed_in,
    mesh_in,
    geo_in,
    pair_in,
    square_out,
):
    feature_width = embed_in.shape[1]
    outgoing_ids = grid_send[0]
    pre_act = jnp.dot(grid_feat, embed_in, preferred_element_type=jnp.float32)
    grid_latent = two_layer(pre_act, square_out[0]).astype(jnp.bfloat16)
    outgoing = grid_latent[outgoing_ids]
    arrived = []
    for offset_id, (lat_step, lon_step) in enumerate(GRID_OFFSETS):
        if lat_step != 0:
            moved = from_behind(outgoing[offset_id], "lat", lat_step)
        else:
            moved = from_behind_2(outgoing[offset_id], "lon", lon_step)
        arrived.append(moved)
    received_grid = jnp.concatenate([grid_latent] + arrived, axis=0)
    sender_term = jnp.dot(received_grid, pair_in[0, 0], preferred_element_type=jnp.float32)
    mesh_first = jnp.dot(mesh_geom.T, mesh_in, precision=lax.Precision.HIGHEST)
    mesh_start = two_layer(mesh_first, square_out[1]).astype(jnp.bfloat16)
    receiver_term = jnp.dot(mesh_start, pair_in[0, 1], preferred_element_type=jnp.float32)
    edge_sum = edge_sums(
        sender_term, receiver_term, g2m_sender, g2m_receiver, g2m_geom, geo_in[0], square_out[2]
    )
    mesh_latent = node_update(mesh_start, edge_sum, pair_in[0], square_out[3])
    near_ids = mesh_adjacent_lists[0]
    far_ids = mesh_far[0]
    for section_id in range(1, geo_in.shape[0]):
        near_out = mesh_latent[near_ids]
        banded = {}
        for lat_step in (-1, 1):
            first = 0 if lat_step < 0 else 5
            banded[lat_step] = from_behind(near_out[first : first + 3], "lat", lat_step)
        columns = {}
        for lon_step in (-1, 1):
            side = 0 if lon_step < 0 else 2
            own_slot = 3 if lon_step < 0 else 4
            stacked = jnp.stack([near_out[own_slot], banded[-1][side], banded[1][side]], axis=0)
            columns[lon_step] = from_behind_2(stacked, "lon", lon_step)
        near_blocks = [
            columns[-1][1],
            banded[-1][1],
            columns[1][1],
            columns[-1][0],
            columns[1][0],
            columns[-1][2],
            banded[1][1],
            columns[1][2],
        ]
        far_out = mesh_latent[far_ids]
        far_in = lax.all_to_all(far_out, ("lat", "lon"), split_axis=0, concat_axis=0, tiled=True)
        sender_table = jnp.concatenate(
            [mesh_latent] + near_blocks + [far_in.reshape(-1, feature_width)], axis=0
        )
        sender_term = jnp.dot(
            sender_table, pair_in[section_id, 0], preferred_element_type=jnp.float32
        )
        receiver_term = jnp.dot(
            mesh_latent, pair_in[section_id, 1], preferred_element_type=jnp.float32
        )
        edge_sum = edge_sums(
            sender_term,
            receiver_term,
            mesh_sender,
            mesh_receiver,
            mesh_edge_geom,
            geo_in[section_id],
            square_out[2 + 2 * section_id],
        )
        mesh_latent = node_update(
            mesh_latent, edge_sum, pair_in[section_id], square_out[3 + 2 * section_id]
        )
    return mesh_latent


def solution(mesh):
    in_specs = (
        P(("lat", "lon"), None),
        P(("lat", "lon"), None, None),
        P(("lat", "lon")),
        P(("lat", "lon")),
        P(None, ("lat", "lon")),
        P(None, ("lat", "lon")),
        P(("lat", "lon"), None, None),
        P(("lat", "lon"), None, None),
        P(("lat", "lon")),
        P(("lat", "lon")),
        P(None, ("lat", "lon")),
        P(),
        P(),
        P(),
        P(),
        P(),
    )
    out_specs = P(("lat", "lon"), None)
    return jax.shard_map(
        per_device, mesh=mesh, in_specs=in_specs, out_specs=out_specs, check_vma=False
    )
```

profile of v0, /device:TPU:6, one launch (start us, length us, event | category | flops | bytes accessed | tf_op | source)
XLA Modules:
  0.0 325.6 jit_solution(14074189624154669967)
XLA Ops:
  1.2 2.8 fusion.109
  4.3 1.8 constant_dynamic-update-slice_fusion.4
  6.1 1.5 copy.22
  7.6 4.0 %gather_fusion = bf16[1024,512]{1,0:T(8,128)(2,1)S(1)} fusion(bf16[1024,512]{1,0:T(8,128)(2,1)S(1)} %copy.22, s32[1024]{0:T(1024)S(1)} %broadcast_clamp_fusion), kind=kCustom, calls=%fused_computation | custom fusion | bytes 2101248 | tf_op jit(solution)/shard_map/gather | solution.py:75
  12.6 2.7 collective-permute-start
  16.1 5.2 %collective-permute-start.1 = (bf16[256,512]{0,1:T(8,128)(2,1)}, bf16[256,512]{0,1:T(8,128)(2,1)}, u32[]{:S(2)}, u32[]{:S(2)}) collective-permute-start(bf16[256,512]{0,1:T(8,128)(2,1)} %copy.29), channel_id=1, source_target_pairs={{0,8},{8,16},{16,24},{24,32},{32,40},{40,48},{48,56},{56,64},{64,7... | collective-permute-start | bytes 786440 | tf_op jit(solution)/shard_map/ppermute | solution.py:13
  21.5 1.9 collective-permute-start.2
  24.4 1.5 fusion.110
  29.2 9.9 %fusion.94 = f32[4096,512]{1,0:T(8,128)} fusion(f32[4,4096]{1,0:T(4,128)S(1)} %copy-done.11, f32[3,4,512]{2,1,0:T(4,128)} %param.29), kind=kOutput, calls=%fused_computation.176 | convolution fusion | flops 100663296 | bytes 8462336 | tf_op jit(solution)/shard_map/dot_general | solution.py:36
  40.0 16.8 %gather_fusion.2 = f32[4096,512]{1,0:T(8,128)} fusion(f32[320,512]{1,0:T(8,128)S(1)} %fusion.43, s32[4096]{0:T(1024)S(1)} %get-tuple-element.48), kind=kCustom, calls=%fused_computation.2 | custom fusion | bytes 16793600 | tf_op jit(solution)/shard_map/gather | solution.py:37
  57.6 1.7 constant_dynamic-update-slice_fusion.2
  60.8 4.9 %fusion.45 = f32[2048,512]{1,0:T(8,128)} fusion(bf16[2048,512]{0,1:T(8,128)(2,1)} %constant_dynamic-update-slice_fusion, bf16[3,4,512,512]{3,2,1,0:T(8,128)(2,1)} %param.30), kind=kOutput, calls=%fused_computation.85 | convolution fusion | flops 1073741824 | bytes 6815744 | tf_op jit(solution)/shard_map/dot_general | solution.py:84
  65.8 20.2 %gather_fusion.1 = f32[4096,512]{1,0:T(8,128)} fusion(f32[2048,512]{1,0:T(8,128)} %fusion.45, s32[4096]{0:T(1024)S(1)} %get-tuple-element.47), kind=kCustom, calls=%fused_computation.1 | custom fusion | bytes 16793600 | tf_op jit(solution)/shard_map/gather | solution.py:37
  86.0 10.1 %fusion.111 = (f32[4096]{0:T(1024)S(1)}, f32[4096,512]{0,1:T(8,128)S(1)}) fusion(bf16[8,512,512]{2,1,0:T(8,128)(2,1)} %param.31, f32[4096,512]{1,0:T(8,128)} %gather_fusion.2, f32[4096,512]{1,0:T(8,128)} %fusion.94, f32[4096,512]{1,0:T(8,128)} %gather_fusion.1), kind=kOutput, calls=%fused_computation.210 | convolution fusion | flops 2164256768 | bytes 34095104 | tf_op jit(solution)/shard_map/dot_general | solution.py:30
  97.1 2.2 copy-done.8
  99.4 5.4 %multiply_convert_fusion.31 = bf16[320,512]{1,0:T(8,128)(2,1)S(1)} fusion(f32[320,512]{1,0:T(8,128)S(1)} %fusion.48, f32[4096,512]{0,1:T(8,128)} %copy-done.8, f32[4096]{0:T(1024)S(1)} %add_rsqrt_fusion.2, f32[4096]{0:T(1024)S(1)} %broadcast_multiply_fusion.2, s32[4096]{0:T(1024)S(1)} %copy-done.17, bf16[3,4,512,512]{3,2,1,0:T(8,128)(2,1)} %param.30), kind=kOutput, calls=%fused_computation.53 | convolution fusion | flops 1518698496 | bytes 9945088 | tf_op jit(solution)/shard_map/dot_general | solution.py:47
  107.5 3.5 %gather_fusion.3 = bf16[896,512]{1,0:T(8,128)(2,1)S(1)} fusion(bf16[320,512]{1,0:T(8,128)(2,1)S(1)} %get-tuple-element.8, s32[1024]{0:T(1024)S(1)} %get-tuple-element.52), kind=kCustom, calls=%fused_computation.3 | custom fusion | bytes 1838592 | tf_op jit(solution)/shard_map/gather | solution.py:95
  111.8 2.1 collective-permute-start.4
  115.3 6.0 %collective-permute-start.5 = (bf16[3,112,512]{2,1,0:T(8,128)(2,1)S(1)}, bf16[3,112,512]{2,1,0:T(8,128)(2,1)S(1)}, u32[]{:S(2)}, u32[]{:S(2)}) collective-permute-start(bf16[3,112,512]{2,1,0:T(8,128)(2,1)S(1)} %bitcast.198), channel_id=1, source_target_pairs={{0,8},{8,16},{16,24},{24,32},{32,40},{40,48},{48,56},{56,64},{64,7... | collective-permute-start | bytes 1032200 | tf_op jit(solution)/shard_map/ppermute | solution.py:13
  121.4 2.0 gather_fusion.4
  124.3 9.2 %all-to-all-start = ((bf16[128,4,512]{2,1,0:T(4,128)(2,1)}), bf16[128,4,512]{2,1,0:T(4,128)(2,1)S(1)}, u32[]{:S(2)}, u32[]{:S(2)}) async-start(bf16[128,4,512]{2,1,0:T(4,128)(2,1)} %reshape.235), calls=%async_computation | async-start | bytes 1048576 | tf_op jit(solution)/shard_map/all_to_all | solution.py:117
  133.6 16.8 %gather_fusion.6 = f32[4096,512]{1,0:T(8,128)} fusion(f32[320,512]{1,0:T(8,128)S(1)} %fusion.33, s32[4096]{0:T(1024)S(1)} %get-tuple-element.50), kind=kCustom, calls=%fused_computation.6 | custom fusion | bytes 16793600 | tf_op jit(solution)/shard_map/gather | solution.py:37
  151.2 2.5 collective-permute-start.6
  153.7 2.2 fusion.37
  156.9 1.9 collective-permute-done.6
  160.1 4.7 %collective-permute-done.7 = bf16[3,112,512]{2,1,0:T(8,128)(2,1)S(1)} collective-permute-done((bf16[3,112,512]{2,1,0:T(8,128)(2,1)}, bf16[3,112,512]{2,1,0:T(8,128)(2,1)S(1)}, u32[]{:S(2)}, u32[]{:S(2)}) %collective-permute-start.7) | collective-permute-done | bytes 344096 | tf_op jit(solution)/shard_map/ppermute | solution.py:19
  169.5 2.6 fusion.35
  172.2 18.0 %gather_fusion.5 = f32[4096,512]{1,0:T(8,128)} fusion(f32[1728,512]{1,0:T(8,128)S(1)} %fusion.35, s32[4096]{0:T(1024)} %get-tuple-element.49), kind=kCustom, calls=%fused_computation.5 | custom fusion | bytes 16793600 | tf_op jit(solution)/shard_map/gather | solution.py:37
  190.2 13.5 %multiply_convert_fusion.3 = bf16[4096,512]{1,0:T(8,128)(2,1)S(1)} fusion(f32[4096,512]{1,0:T(8,128)} %gather_fusion.6, f32[4096,512]{1,0:T(8,128)} %gather_fusion.5, f32[4,4096]{1,0:T(4,128)} %param.26, f32[3,4,512]{2,1,0:T(4,128)} %param.29), kind=kOutput, calls=%fused_computation.16 | convolution fusion | flops 115343360 | bytes 21045248 | tf_op jit(solution)/shard_map/dot_general | solution.py:36
  203.7 3.5 %fusion.113 = (f32[4096]{0:T(1024)S(1)}, f32[4096,512]{0,1:T(8,128)S(1)}) fusion(bf16[4096,512]{1,0:T(8,128)(2,1)S(1)} %multiply_convert_fusion.3, bf16[8,512,512]{2,1,0:T(8,128)(2,1)} %param.31), kind=kOutput, calls=%fused_computation.212 | convolution fusion | flops 2149576704 | bytes 13123584 | tf_op jit(solution)/shard_map/dot_general | solution.py:30
  208.3 2.2 copy-done.6
  210.5 5.5 %multiply_convert_fusion.28 = bf16[320,512]{1,0:T(8,128)(2,1)S(1)} fusion(f32[320,512]{1,0:T(8,128)S(1)} %copy-done.9, f32[4096,512]{0,1:T(8,128)} %copy-done.6, f32[4096]{0:T(1024)S(1)} %add_rsqrt_fusion.1, f32[4096]{0:T(1024)S(1)} %broadcast_multiply_fusion.1, s32[4096]{0:T(1024)S(1)} %copy-done.19, bf16[3,4,512,512]{3,2,1,0:T(8,128)(2,1)} %param.30), kind=kOutput, calls=%fused_computation.50 | convolution fusion | flops 1518698496 | bytes 9945088 | tf_op jit(solution)/shard_map/dot_general | solution.py:47
  218.7 3.5 %gather_fusion.7 = bf16[896,512]{1,0:T(8,128)(2,1)S(1)} fusion(bf16[320,512]{1,0:T(8,128)(2,1)S(1)} %get-tuple-element.6, s32[1024]{0:T(1024)S(1)} %get-tuple-element.52), kind=kCustom, calls=%fused_computation.7 | custom fusion | bytes 1838592 | tf_op jit(solution)/shard_map/gather | solution.py:95
  222.3 2.7 collective-permute-start.8
  226.4 5.2 %collective-permute-start.9 = (bf16[3,112,512]{2,1,0:T(8,128)(2,1)S(1)}, bf16[3,112,512]{2,1,0:T(8,128)(2,1)S(1)}, u32[]{:S(2)}, u32[]{:S(2)}) collective-permute-start(bf16[3,112,512]{2,1,0:T(8,128)(2,1)S(1)} %bitcast.197), channel_id=1, source_target_pairs={{0,8},{8,16},{16,24},{24,32},{32,40},{40,48},{48,56},{56,64},{64,7... | collective-permute-start | bytes 1032200 | tf_op jit(solution)/shard_map/ppermute | solution.py:13
  231.6 2.0 gather_fusion.8
  234.6 7.6 %all-to-all-start.1 = ((bf16[128,4,512]{2,1,0:T(4,128)(2,1)}), bf16[128,4,512]{2,1,0:T(4,128)(2,1)S(1)}, u32[]{:S(2)}, u32[]{:S(2)}) async-start(bf16[128,4,512]{2,1,0:T(4,128)(2,1)} %reshape.267), calls=%async_computation.1 | async-start | bytes 1048576 | tf_op jit(solution)/shard_map/all_to_all | solution.py:117
  242.2 16.8 %gather_fusion.10 = f32[4096,512]{1,0:T(8,128)} fusion(f32[320,512]{1,0:T(8,128)S(1)} %fusion.22, s32[4096]{0:T(1024)S(1)} %copy-done.14), kind=kCustom, calls=%fused_computation.10 | custom fusion | bytes 16793600 | tf_op jit(solution)/shard_map/gather | solution.py:37
  259.1 2.5 collective-permute-start.10
  261.6 2.2 fusion.26
  264.8 1.6 collective-permute-done.10
  267.7 5.0 %collective-permute-done.11 = bf16[3,112,512]{2,1,0:T(8,128)(2,1)S(1)} collective-permute-done((bf16[3,112,512]{2,1,0:T(8,128)(2,1)}, bf16[3,112,512]{2,1,0:T(8,128)(2,1)S(1)}, u32[]{:S(2)}, u32[]{:S(2)}) %collective-permute-start.11) | collective-permute-done | bytes 344096 | tf_op jit(solution)/shard_map/ppermute | solution.py:19
  277.5 2.7 fusion.24
  280.1 16.8 %gather_fusion.9 = f32[4096,512]{1,0:T(8,128)} fusion(f32[1728,512]{1,0:T(8,128)S(1)} %fusion.24, s32[4096]{0:T(1024)S(1)} %copy-done.12), kind=kCustom, calls=%fused_computation.9 | custom fusion | bytes 16793600 | tf_op jit(solution)/shard_map/gather | solution.py:37
  296.9 13.4 %multiply_convert_fusion.1 = bf16[4096,512]{1,0:T(8,128)(2,1)S(1)} fusion(f32[4096,512]{1,0:T(8,128)} %gather_fusion.10, f32[4096,512]{1,0:T(8,128)} %gather_fusion.9, f32[4,4096]{1,0:T(4,128)} %param.26, f32[3,4,512]{2,1,0:T(4,128)} %param.29), kind=kOutput, calls=%fused_computation.13 | convolution fusion | flops 115343360 | bytes 21045248 | tf_op jit(solution)/shard_map/dot_general | solution.py:36
  310.3 3.5 %fusion.115 = (f32[4096]{0:T(1024)S(1)}, f32[4096,512]{0,1:T(8,128)S(1)}) fusion(bf16[4096,512]{1,0:T(8,128)(2,1)S(1)} %multiply_convert_fusion.1, bf16[8,512,512]{2,1,0:T(8,128)(2,1)} %param.31), kind=kOutput, calls=%fused_computation.214 | convolution fusion | flops 2149576704 | bytes 13123584 | tf_op jit(solution)/shard_map/dot_general | solution.py:30
  315.0 2.2 copy-done.7
  317.2 5.5 %multiply_convert_fusion.25 = bf16[320,512]{1,0:T(8,128)(2,1)S(1)} fusion(f32[320,512]{1,0:T(8,128)S(1)} %copy-done.10, f32[4096,512]{0,1:T(8,128)} %copy-done.7, f32[4096]{0:T(1024)S(1)} %add_rsqrt_fusion, f32[4096]{0:T(1024)S(1)} %broadcast_multiply_fusion, s32[4096]{0:T(1024)S(1)} %copy-done.20, bf16[3,4,512,512]{3,2,1,0:T(8,128)(2,1)} %param.30), kind=kOutput, calls=%fused_computation.47 | convolution fusion | flops 1518698496 | bytes 9945088 | tf_op jit(solution)/shard_map/dot_general | solution.py:47
  (150 shorter events, 42.3 us)
Async XLA Ops:
  0.0 1.2 copy-start
  4.0 3.6 %copy-start.21 = (s32[1,4,256]{2,1,0:T(4,128)S(1)}, s32[1,4,256]{2,1,0:T(4,128)}, u32[]{:S(2)}) copy-start(s32[1,4,256]{2,1,0:T(4,128)} %param.17) | copy-start | bytes 12292
  11.6 12.0 %copy-start.24 = (f32[3,512]{1,0:T(4,128)S(1)}, f32[3,512]{1,0:T(4,128)}, u32[]{:S(2)}) copy-start(f32[3,512]{1,0:T(4,128)} %param.28) | copy-start | bytes 18436
  11.6 12.0 %copy-start.25 = (f32[3,320]{1,0:T(4,128)S(1)}, f32[3,320]{1,0:T(4,128)}, u32[]{:S(2)}) copy-start(f32[3,320]{1,0:T(4,128)} %param.21) | copy-start | bytes 11524
  12.6 44.2 %collective-permute-start = (bf16[256,512]{0,1:T(8,128)(2,1)}, bf16[256,512]{0,1:T(8,128)(2,1)S(1)}, u32[]{:S(2)}, u32[]{:S(2)}) collective-permute-start(bf16[256,512]{0,1:T(8,128)(2,1)} %copy.28), channel_id=1, source_target_pairs={{8,0},{16,8},{24,16},{32,24},{40,32},{48,40},{56,48},{64,56},{72,6... | collective-permute-start | bytes 786440 | tf_op jit(solution)/shard_map/ppermute | solution.py:13
  16.1 41.4 %collective-permute-start.1 = (bf16[256,512]{0,1:T(8,128)(2,1)}, bf16[256,512]{0,1:T(8,128)(2,1)}, u32[]{:S(2)}, u32[]{:S(2)}) collective-permute-start(bf16[256,512]{0,1:T(8,128)(2,1)} %copy.29), channel_id=1, source_target_pairs={{0,8},{8,16},{16,24},{24,32},{32,40},{40,48},{48,56},{56,64},{64,7... | collective-permute-start | bytes 786440 | tf_op jit(solution)/shard_map/ppermute | solution.py:13
  21.5 37.8 %collective-permute-start.2 = (bf16[256,512]{0,1:T(8,128)(2,1)S(1)}, bf16[256,512]{0,1:T(8,128)(2,1)S(1)}, u32[]{:S(2)}, u32[]{:S(2)}) collective-permute-start(bf16[256,512]{0,1:T(8,128)(2,1)S(1)} %copy.30), channel_id=1, source_target_pairs={{1,0},{2,1},{3,2},{4,3},{5,4},{6,5},{7,6},{0,7},{9,8},{10,9},{11,1... | collective-permute-start | bytes 786440 | tf_op jit(solution)/shard_map/ppermute | solution.py:19
  23.5 5.5 %copy-start.22 = (s32[1,8,112]{2,1,0:T(8,128)S(1)}, s32[1,8,112]{2,1,0:T(8,128)}, u32[]{:S(2)}) copy-start(s32[1,8,112]{2,1,0:T(8,128)} %param.22) | copy-start | bytes 10756
  23.6 5.5 %copy-start.15 = (s32[4096]{0:T(1024)S(1)}, s32[4096]{0:T(1024)}, u32[]{:S(2)}) copy-start(s32[4096]{0:T(1024)} %param.18) | copy-start | bytes 49156
  23.6 5.5 %copy-start.17 = (s32[4096]{0:T(1024)S(1)}, s32[4096]{0:T(1024)}, u32[]{:S(2)}) copy-start(s32[4096]{0:T(1024)} %param.19) | copy-start | bytes 49156
  23.6 5.5 %copy-start.11 = (f32[4,4096]{1,0:T(4,128)S(1)}, f32[4,4096]{1,0:T(4,128)}, u32[]{:S(2)}) copy-start(f32[4,4096]{1,0:T(4,128)} %param.20) | copy-start | bytes 196612
  23.6 36.4 %collective-permute-start.3 = (bf16[256,512]{0,1:T(8,128)(2,1)S(1)}, bf16[256,512]{0,1:T(8,128)(2,1)S(1)}, u32[]{:S(2)}, u32[]{:S(2)}) collective-permute-start(bf16[256,512]{0,1:T(8,128)(2,1)S(1)} %copy.31), channel_id=1, source_target_pairs={{7,0},{0,1},{1,2},{2,3},{3,4},{4,5},{5,6},{6,7},{15,8},{8,9},{9,10... | collective-permute-start | bytes 786440 | tf_op jit(solution)/shard_map/ppermute | solution.py:19
  29.1 10.0 %copy-start.16 = (s32[4096]{0:T(1024)S(1)}, s32[4096]{0:T(1024)}, u32[]{:S(2)}) copy-start(s32[4096]{0:T(1024)} %param.24) | copy-start | bytes 49156
  29.1 9.9 %copy-start.18 = (s32[4096]{0:T(1024)S(1)}, s32[4096]{0:T(1024)}, u32[]{:S(2)}) copy-start(s32[4096]{0:T(1024)} %param.25) | copy-start | bytes 49156
  29.2 10.5 %copy-start.23 = (s32[1,128,4]{1,2,0:T(4,128)S(1)}, s32[1,128,4]{1,2,0:T(4,128)}, u32[]{:S(2)}) copy-start(s32[1,128,4]{1,2,0:T(4,128)} %param.23) | copy-start | bytes 6148
  39.7 93.9 %copy-start.13 = (s32[4096]{0:T(1024)}, s32[4096]{0:T(1024)S(1)}, u32[]{:S(2)}) copy-start(s32[4096]{0:T(1024)S(1)} %get-tuple-element.50) | copy-start | bytes 49156
  96.1 3.2 copy-start.8
  107.5 46.2 %copy-start.2 = (bf16[320,512]{1,0:T(8,128)(2,1)}, bf16[320,512]{1,0:T(8,128)(2,1)S(1)}, u32[]{:S(2)}) copy-start(bf16[320,512]{1,0:T(8,128)(2,1)S(1)} %get-tuple-element.8) | copy-start | bytes 983044
  111.8 38.5 %collective-permute-start.4 = (bf16[3,112,512]{2,1,0:T(8,128)(2,1)}, bf16[3,112,512]{2,1,0:T(8,128)(2,1)S(1)}, u32[]{:S(2)}, u32[]{:S(2)}) collective-permute-start(bf16[3,112,512]{2,1,0:T(8,128)(2,1)} %bitcast.14), channel_id=1, source_target_pairs={{8,0},{16,8},{24,16},{32,24},{40,32},{48,40},{56,48},{64,56},{72,6... | collective-permute-start | bytes 1032200 | tf_op jit(solution)/shard_map/ppermute | solution.py:13
  115.3 35.1 %collective-permute-start.5 = (bf16[3,112,512]{2,1,0:T(8,128)(2,1)S(1)}, bf16[3,112,512]{2,1,0:T(8,128)(2,1)S(1)}, u32[]{:S(2)}, u32[]{:S(2)}) collective-permute-start(bf16[3,112,512]{2,1,0:T(8,128)(2,1)S(1)} %bitcast.198), channel_id=1, source_target_pairs={{0,8},{8,16},{16,24},{24,32},{32,40},{40,48},{48,56},{56,64},{64,7... | collective-permute-start | bytes 1032200 | tf_op jit(solution)/shard_map/ppermute | solution.py:13
  124.3 32.4 %all-to-all-start = ((bf16[128,4,512]{2,1,0:T(4,128)(2,1)}), bf16[128,4,512]{2,1,0:T(4,128)(2,1)S(1)}, u32[]{:S(2)}, u32[]{:S(2)}) async-start(bf16[128,4,512]{2,1,0:T(4,128)(2,1)} %reshape.235), calls=%async_computation | async-start | bytes 1048576 | tf_op jit(solution)/shard_map/all_to_all | solution.py:117
  151.2 7.6 %collective-permute-start.6 = (bf16[3,112,512]{2,1,0:T(8,128)(2,1)}, bf16[3,112,512]{2,1,0:T(8,128)(2,1)S(1)}, u32[]{:S(2)}, u32[]{:S(2)}) collective-permute-start(bf16[3,112,512]{2,1,0:T(8,128)(2,1)} %pad_maximum_fusion), channel_id=1, source_target_pairs={{1,0},{2,1},{3,2},{4,3},{5,4},{6,5},{7,6},{0,7},{9,8},{10,9},{11,1... | collective-permute-start | bytes 1032200 | tf_op jit(solution)/shard_map/ppermute | solution.py:19
  156.7 8.1 %collective-permute-start.7 = (bf16[3,112,512]{2,1,0:T(8,128)(2,1)}, bf16[3,112,512]{2,1,0:T(8,128)(2,1)S(1)}, u32[]{:S(2)}, u32[]{:S(2)}) collective-permute-start(bf16[3,112,512]{2,1,0:T(8,128)(2,1)} %pad_maximum_fusion.1), channel_id=1, source_target_pairs={{7,0},{0,1},{1,2},{2,3},{3,4},{4,5},{5,6},{6,7},{15,8},{8,9},{9,10... | collective-permute-start | bytes 1032200 | tf_op jit(solution)/shard_map/ppermute | solution.py:19
  207.2 3.2 copy-start.6
  207.3 3.2 copy-start.9
  207.3 3.2 copy-start.19
  210.5 7.2 %copy-start.3 = (bf16[320,512]{1,0:T(8,128)(2,1)S(1)}, bf16[320,512]{1,0:T(8,128)(2,1)}, u32[]{:S(2)}) copy-start(bf16[320,512]{1,0:T(8,128)(2,1)} %copy-done.2) | copy-start | bytes 983044
  218.7 43.0 %copy-start.4 = (bf16[320,512]{1,0:T(8,128)(2,1)}, bf16[320,512]{1,0:T(8,128)(2,1)S(1)}, u32[]{:S(2)}) copy-start(bf16[320,512]{1,0:T(8,128)(2,1)S(1)} %get-tuple-element.6) | copy-start | bytes 983044
  222.3 19.9 %copy-start.14 = (s32[4096]{0:T(1024)S(1)}, s32[4096]{0:T(1024)}, u32[]{:S(2)}) copy-start(s32[4096]{0:T(1024)} %copy-done.13) | copy-start | bytes 49156
  222.3 36.8 %collective-permute-start.8 = (bf16[3,112,512]{2,1,0:T(8,128)(2,1)S(1)}, bf16[3,112,512]{2,1,0:T(8,128)(2,1)S(1)}, u32[]{:S(2)}, u32[]{:S(2)}) collective-permute-start(bf16[3,112,512]{2,1,0:T(8,128)(2,1)S(1)} %bitcast.199), channel_id=1, source_target_pairs={{8,0},{16,8},{24,16},{32,24},{40,32},{48,40},{56,48},{64,56},{72,6... | collective-permute-start | bytes 1032200 | tf_op jit(solution)/shard_map/ppermute | solution.py:13
  226.4 32.6 %collective-permute-start.9 = (bf16[3,112,512]{2,1,0:T(8,128)(2,1)S(1)}, bf16[3,112,512]{2,1,0:T(8,128)(2,1)S(1)}, u32[]{:S(2)}, u32[]{:S(2)}) collective-permute-start(bf16[3,112,512]{2,1,0:T(8,128)(2,1)S(1)} %bitcast.197), channel_id=1, source_target_pairs={{0,8},{8,16},{16,24},{24,32},{32,40},{40,48},{48,56},{56,64},{64,7... | collective-permute-start | bytes 1032200 | tf_op jit(solution)/shard_map/ppermute | solution.py:13
  234.6 30.1 %all-to-all-start.1 = ((bf16[128,4,512]{2,1,0:T(4,128)(2,1)}), bf16[128,4,512]{2,1,0:T(4,128)(2,1)S(1)}, u32[]{:S(2)}, u32[]{:S(2)}) async-start(bf16[128,4,512]{2,1,0:T(4,128)(2,1)} %reshape.267), calls=%async_computation.1 | async-start | bytes 1048576 | tf_op jit(solution)/shard_map/all_to_all | solution.py:117
  259.1 7.3 %collective-permute-start.10 = (bf16[3,112,512]{2,1,0:T(8,128)(2,1)S(1)}, bf16[3,112,512]{2,1,0:T(8,128)(2,1)S(1)}, u32[]{:S(2)}, u32[]{:S(2)}) collective-permute-start(bf16[3,112,512]{2,1,0:T(8,128)(2,1)S(1)} %pad_maximum_fusion.2), channel_id=1, source_target_pairs={{1,0},{2,1},{3,2},{4,3},{5,4},{6,5},{7,6},{0,7},{9,8},{10,9},{11,1... | collective-permute-start | bytes 1032200 | tf_op jit(solution)/shard_map/ppermute | solution.py:19
  264.6 8.1 %collective-permute-start.11 = (bf16[3,112,512]{2,1,0:T(8,128)(2,1)}, bf16[3,112,512]{2,1,0:T(8,128)(2,1)S(1)}, u32[]{:S(2)}, u32[]{:S(2)}) collective-permute-start(bf16[3,112,512]{2,1,0:T(8,128)(2,1)} %pad_maximum_fusion.3), channel_id=1, source_target_pairs={{7,0},{0,1},{1,2},{2,3},{3,4},{4,5},{5,6},{6,7},{15,8},{8,9},{9,10... | collective-permute-start | bytes 1032200 | tf_op jit(solution)/shard_map/ppermute | solution.py:19
  277.5 2.7 copy-start.12
  313.9 3.2 copy-start.7
  313.9 3.2 copy-start.10
  313.9 3.2 copy-start.20
  317.2 7.3 %copy-start.5 = (bf16[320,512]{1,0:T(8,128)(2,1)S(1)}, bf16[320,512]{1,0:T(8,128)(2,1)}, u32[]{:S(2)}) copy-start(bf16[320,512]{1,0:T(8,128)(2,1)} %copy-done.4) | copy-start | bytes 983044
  317.2 8.2 %copy-start.1 = (bf16[1024,474]{0,1:T(8,128)(2,1)S(1)}, bf16[1024,474]{0,1:T(8,128)(2,1)}, u32[]{:S(2)}) copy-start(bf16[1024,474]{0,1:T(8,128)(2,1)} %param.16) | copy-start | bytes 2912260
where the time goes:
time: 331 us; the launch traced here: 326 us
  local copies, waits for them, and re-layouts  151 us (46%)
  matrix products  100 us (30%)
  starting transfers between devices  47.8 us (14%)
  waiting for transfers between devices  13.3 us (4%)
  other arithmetic  12 us (4%)
    gather x6, local copies, waits for them, and re-layouts, edge_sums(): pre_act = pre_act + sender_term[senders] + receiver_term[row_ids]  105 us
    dot_general x3, matrix products, edge_sums(): pre_act = jnp.dot(geometry.T, geo_weight, precision=lax.Precision.HIGHEST)  36.8 us
    dot_general x8, matrix products, two_layer(): jnp.dot(hidden, out_weight, preferred_element_type=jnp.float32)  25.9 us
    ppermute x6, starting transfers between devices, from_behind(): return lax.ppermute(block, axis, route)  24 us
    unnamed x76, local copies, waits for them, and re-layouts  23.5 us
    all_to_all x2, starting transfers between devices, per_device(): lax.all_to_all(far_out, ('lat', 'lon'), split_axis=0, concat_axis=0, tile...  16.8 us
    dot_general x3, matrix products, node_update(): jnp.dot(edge_sum.astype(jnp.bfloat16), section_weights[3], preferred_elem...  16.5 us
    ppermute x6, waiting for transfers between devices, from_behind_2(): return lax.ppermute(block, axis, route)  13.3 us
  transfers between devices with their start and end apart: 14, of which 4 were waited for; matrix products, arithmetic and copies ran while one was open for 27% of the time, Pallas kernels for 0%

commit v1 on v0

v1 whole, which is shorter than its diff:
```python
import jax
import jax.numpy as jnp
from jax import lax
from jax.experimental import pallas as pl
from jax.experimental.pallas import tpu as pltpu
from jax.sharding import PartitionSpec as P

EPSILON = 1e-05
GRID_OFFSETS = ((-1, 0), (1, 0), (0, -1), (0, 1))
MESH_OFFSETS = ((-1, -1), (-1, 0), (-1, 1), (0, -1), (0, 1), (1, -1), (1, 0), (1, 1))
N_LAT, N_LON = 16, 8
DEVICES = N_LAT * N_LON
D = 512
LANES = 128
PARTS = D // LANES
C_IN = 474
GRID_DEV = 1024
GSLOT = 256
NODES = 320
NEAR = 112
FAR = 4
EDGES = 4096
CHUNK = 512
KX = NODES + 16
NEAR_ROWS = 8 * NEAR
MESH_AXES = pl.DeviceIdType.MESH
BF16, F32 = jnp.bfloat16, jnp.float32


def matmul(left, right):
    return jnp.dot(left, right, preferred_element_type=F32)


def silu(x):
    half = 0.5 * x
    return half * jnp.tanh(half) + half


def layer_norm(values):
    centre = values - jnp.sum(values, axis=-1, keepdims=True) * (1.0 / D)
    spread = jnp.sum(centre * centre, axis=-1, keepdims=True) * (1.0 / D)
    return centre * lax.rsqrt(spread + EPSILON)


def split_high_low(values):
    high = values.astype(BF16).astype(F32)
    return high, (values - high).astype(BF16).astype(F32)


def store_rows(table, first, values):
    rows = values.shape[0]
    for part in range(PARTS):
        table[pl.ds(first * PARTS + part, rows, stride=PARTS), :] = values[
            :, part * LANES : (part + 1) * LANES
        ]


def load_rows(table, first, rows):
    return jnp.concatenate(
        [table[pl.ds(first * PARTS + part, rows, stride=PARTS), :] for part in range(PARTS)],
        axis=1,
    )


def kernel(
    grid_send, g2m_sender, near_lists, far_lists, mesh_sender,
    g2m_receiver, g2m_geom, mesh_geom, mesh_receiver, mesh_edge_geom, mesh_in, geo_in,
    grid_hbm, embed_hbm, pair_hbm, square_hbm,
    out,
    grid, embed, pair, square,
    table, staged, grid_out, grid_arrived, near_out, near_arrived, far_out, far_arrived,
    geo_x, geo_w, x_grid, x_mesh, y_rows, pre, gathered, hidden, edge_sum, latent,
    load_sem, grid_ssem, grid_rsem, near_ssem, near_rsem, far_ssem, far_rsem,
):
    lat = lax.axis_index("lat")
    lon = lax.axis_index("lon")
    me = lat * N_LON + lon

    loads = [
        pltpu.make_async_copy(grid_hbm, grid, load_sem.at[0]),
        pltpu.make_async_copy(embed_hbm, embed, load_sem.at[1]),
        pltpu.make_async_copy(square_hbm, square, load_sem.at[2]),
        pltpu.make_async_copy(pair_hbm, pair, load_sem.at[3]),
    ]
    for load in loads:
        load.start()

    barrier = pltpu.get_barrier_semaphore()

    def greet(step, carry):
        other = lax.rem(me + step, DEVICES)
        pl.semaphore_signal(
            barrier, inc=1, device_id=(other // N_LON, lax.rem(other, N_LON)),
            device_id_type=MESH_AXES,
        )
        return carry

    lax.fori_loop(1, DEVICES, greet, 0)

    def send_to(offset, source, target, ssem, rsem):
        lat_step, lon_step = offset
        there = lat + lat_step
        copy = pltpu.make_async_remote_copy(
            source, target, ssem, rsem,
            device_id=(there, lax.rem(lon + lon_step + N_LON, N_LON)),
            device_id_type=MESH_AXES,
        )
        return copy, jnp.logical_and(there >= 0, there < N_LAT)

    def source_exists(offset):
        here = lat - offset[0]
        return jnp.logical_and(here >= 0, here < N_LAT)

    for load in loads:
        load.wait()
    rows_at_once = 256

    def embed_rows(block, carry):
        rows = pl.ds(pl.multiple_of(block * rows_at_once, rows_at_once), rows_at_once)
        first = silu(matmul(grid[rows, :], embed[...])).astype(BF16)
        grid_latent = layer_norm(matmul(first, square[0])).astype(BF16)
        store_rows(table, block * rows_at_once, matmul(grid_latent, pair[0, 0]))
        return carry

    lax.fori_loop(0, GRID_DEV // rows_at_once, embed_rows, 0)

    def pick(list_ref, first_of, count):
        def some(block, carry):
            for k in range(16):
                slot = block * 16 + k
                row = list_ref(slot)
                staged[pl.ds(pl.multiple_of((first_of + slot) * PARTS, PARTS), PARTS), :] = table[
                    pl.ds(row * PARTS, PARTS), :
                ]
            return carry
        lax.fori_loop(0, count // 16, some, 0)

    def run_if(condition, offset, act):
        if offset[0] == 0:
            act()
        else:
            pl.when(condition)(act)

    pl.semaphore_wait(barrier, DEVICES - 1)
    grid_sends = []
    for d, offset in enumerate(GRID_OFFSETS):
        pick(lambda slot, d=d: grid_send[0, d, slot], d * GSLOT, GSLOT)
        grid_out[d] = staged[pl.ds(d * GSLOT * PARTS, GSLOT * PARTS), :].astype(BF16)
        copy, exists = send_to(
            offset, grid_out.at[d], grid_arrived.at[d], grid_ssem.at[d], grid_rsem.at[d]
        )
        run_if(exists, offset, copy.start)
        grid_sends.append((copy, exists, offset))

    def build_x(x_ref, receiver, geometry):
        high, low = split_high_low(geometry[...])
        geo_x[0:4, :] = high
        geo_x[4:8, :] = low
        geo_x[8:12, :] = high
        geo_x[12:16, :] = jnp.zeros((4, EDGES), F32)
        x_ref[NODES:KX, :] = geo_x[...].astype(BF16)

        def some(block, carry):
            columns = pl.ds(pl.multiple_of(block * CHUNK, CHUNK), CHUNK)
            node = lax.broadcasted_iota(jnp.int32, (NODES, CHUNK), 0)
            x_ref[0:NODES, columns] = jnp.where(node == receiver[:, columns], 1.0, 0.0).astype(BF16)
            return carry

        lax.fori_loop(0, EDGES // CHUNK, some, 0)

    def pre_activation(section, x_ref):
        y_rows[0:NODES, :] = matmul(latent[...], pair[section, 1]).astype(BF16)
        high, low = split_high_low(geo_in[section])
        geo_w[0:4, :] = high
        geo_w[4:8, :] = high
        geo_w[8:12, :] = low
        geo_w[12:16, :] = jnp.zeros((4, D), F32)
        y_rows[NODES:KX, :] = geo_w[...].astype(BF16)

        def some(block, carry):
            chunk = pl.ds(pl.multiple_of(block * CHUNK, CHUNK), CHUNK)
            pre[chunk, :] = lax.dot_general(
                x_ref[:, chunk], y_rows[...], (((0,), (0,)), ((), ())), preferred_element_type=F32
            )
            return carry

        lax.fori_loop(0, EDGES // CHUNK, some, 0)

    build_x(x_grid, g2m_receiver, g2m_geom)
    high, low = split_high_low(mesh_geom[...])
    geo_x[0:3, 0:NODES] = high
    geo_x[3:6, 0:NODES] = low
    geo_x[6:9, 0:NODES] = high
    geo_x[9:16, 0:NODES] = jnp.zeros((7, NODES), F32)
    high, low = split_high_low(mesh_in[...])
    geo_w[0:3, :] = high
    geo_w[3:6, :] = high
    geo_w[6:9, :] = low
    geo_w[9:16, :] = jnp.zeros((7, D), F32)
    mesh_first = lax.dot_general(
        geo_x[:, 0:NODES].astype(BF16), geo_w[...].astype(BF16), (((0,), (0,)), ((), ())),
        preferred_element_type=F32,
    )
    latent[...] = layer_norm(matmul(silu(mesh_first).astype(BF16), square[1])).astype(BF16)
    pre_activation(0, x_grid)
    build_x(x_mesh, mesh_receiver, mesh_edge_geom)

    def edges(section, senders, x_ref):
        edge_sum[...] = jnp.zeros((NODES, D), F32)

        def some(block, carry):
            base = block * CHUNK
            chunk = pl.ds(pl.multiple_of(base, CHUNK), CHUNK)

            def gather(group, inner):
                for k in range(32):
                    slot = group * 32 + k
                    row = senders[base + slot]
                    gathered[pl.ds(pl.multiple_of(slot * PARTS, PARTS), PARTS), :] = table[
                        pl.ds(row * PARTS, PARTS), :
                    ]
                return inner

            lax.fori_loop(0, CHUNK // 32, gather, 0)
            hidden[...] = silu(pre[chunk, :] + load_rows(gathered, 0, CHUNK)).astype(BF16)
            message = layer_norm(matmul(hidden[...], square[2 + 2 * section])).astype(BF16)
            edge_sum[...] += matmul(x_ref[0:NODES, chunk], message)
            return carry

        lax.fori_loop(0, EDGES // CHUNK, some, 0)

    def node_update(section):
        before = latent[...]
        first = matmul(before, pair[section, 2]) + matmul(
            edge_sum[...].astype(BF16), pair[section, 3]
        )
        second = layer_norm(matmul(silu(first).astype(BF16), square[3 + 2 * section]))
        return (before.astype(F32) + second).astype(BF16)

    for d, offset in enumerate(GRID_OFFSETS):
        copy = grid_sends[d][0]
        run_if(source_exists(offset), offset, copy.wait_recv)
        table[pl.ds((GRID_DEV + d * GSLOT) * PARTS, GSLOT * PARTS), :] = grid_arrived[d].astype(F32)
    edges(0, g2m_sender, x_grid)
    latent[...] = node_update(0)

    all_sends = list(grid_sends)
    far_waits = []
    for section in (1, 2):
        step = section - 1
        store_rows(table, 0, matmul(latent[...], pair[section, 0]))
        for d in (0, 1, 2, 5, 6, 7, 3, 4):
            offset = MESH_OFFSETS[d]
            pick(lambda slot, d=d: near_lists[0, d, slot], 0, NEAR)
            near_out[step, d] = staged[0 : NEAR * PARTS, :].astype(BF16)
            copy, exists = send_to(
                offset, near_out.at[step, d], near_arrived.at[step, d],
                near_ssem.at[step, d], near_rsem.at[step, d],
            )
            run_if(exists, offset, copy.start)
            all_sends.append((copy, exists, offset))
        pick(lambda slot: far_lists[0, slot // FAR, lax.rem(slot, FAR)], 0, DEVICES * FAR)
        far_out[step] = staged[0 : DEVICES * FAR * PARTS, :].astype(BF16).reshape(
            DEVICES, FAR * PARTS, LANES
        )
        far_arrived[step, me] = far_out[step, me]

        def send_far(k, carry, step=step):
            other = lax.rem(me + k, DEVICES)
            pltpu.make_async_remote_copy(
                far_out.at[step, other], far_arrived.at[step, me],
                far_ssem.at[step], far_rsem.at[step],
                device_id=(other // N_LON, lax.rem(other, N_LON)), device_id_type=MESH_AXES,
            ).start()
            return carry

        lax.fori_loop(1, DEVICES, send_far, 0)
        pre_activation(section, x_mesh)

        for d, offset in enumerate(MESH_OFFSETS):
            copy, exists = send_to(
                offset, near_out.at[step, d], near_arrived.at[step, d],
                near_ssem.at[step, d], near_rsem.at[step, d],
            )
            run_if(source_exists(offset), offset, copy.wait_recv)
            table[pl.ds((NODES + d * NEAR) * PARTS, NEAR * PARTS), :] = near_arrived[step, d].astype(F32)
        far_wait = pltpu.make_async_remote_copy(
            far_out.at[step, pl.ds(0, DEVICES - 1)], far_arrived.at[step, pl.ds(0, DEVICES - 1)],
            far_ssem.at[step], far_rsem.at[step],
            device_id=(lat, lax.rem(lon + 1, N_LON)), device_id_type=MESH_AXES,
        )
        far_wait.wait_recv()
        far_waits.append(far_wait)
        table[pl.ds((NODES + NEAR_ROWS) * PARTS, DEVICES * FAR * PARTS), :] = far_arrived[step].astype(
            F32
        ).reshape(DEVICES * FAR * PARTS, LANES)
        edges(section, mesh_sender, x_mesh)
        latent[...] = node_update(section)

    out[...] = latent[...]
    for copy, exists, offset in all_sends:
        run_if(exists, offset, copy.wait_send)
    for far_wait in far_waits:
        far_wait.wait_send()


def per_device(
    grid_feat, grid_send, g2m_sender, g2m_receiver, g2m_geom, mesh_geom, mesh_adjacent_lists,
    mesh_far, mesh_sender, mesh_receiver, mesh_edge_geom, embed_in, mesh_in, geo_in, pair_in,
    square_out,
):
    smem = pl.BlockSpec(memory_space=pltpu.SMEM)
    vmem = pl.BlockSpec(memory_space=pltpu.VMEM)
    hbm = pl.BlockSpec(memory_space=pl.ANY)
    dma = pltpu.SemaphoreType.DMA
    return pl.pallas_call(
        kernel,
        out_shape=jax.ShapeDtypeStruct((NODES, D), BF16),
        in_specs=[smem] * 5 + [vmem] * 7 + [hbm] * 4,
        out_specs=vmem,
        scratch_shapes=[
            pltpu.VMEM((GRID_DEV, C_IN), BF16),
            pltpu.VMEM((C_IN, D), BF16),
            pltpu.VMEM((3, 4, D, D), BF16),
            pltpu.VMEM((8, D, D), BF16),
            pltpu.VMEM(((GRID_DEV + 4 * GSLOT) * PARTS, LANES), F32),
            pltpu.VMEM((4 * GSLOT * PARTS, LANES), F32),
            pltpu.VMEM((4, GSLOT * PARTS, LANES), BF16),
            pltpu.VMEM((4, GSLOT * PARTS, LANES), BF16),
            pltpu.VMEM((2, 8, NEAR * PARTS, LANES), BF16),
            pltpu.VMEM((2, 8, NEAR * PARTS, LANES), BF16),
            pltpu.VMEM((2, DEVICES, FAR * PARTS, LANES), BF16),
            pltpu.VMEM((2, DEVICES, FAR * PARTS, LANES), BF16),
            pltpu.VMEM((16, EDGES), F32),
            pltpu.VMEM((16, D), F32),
            pltpu.VMEM((KX, EDGES), BF16),
            pltpu.VMEM((KX, EDGES), BF16),
            pltpu.VMEM((KX, D), BF16),
            pltpu.VMEM((EDGES, D), F32),
            pltpu.VMEM((CHUNK * PARTS, LANES), F32),
            pltpu.VMEM((CHUNK, D), BF16),
            pltpu.VMEM((NODES, D), F32),
            pltpu.VMEM((NODES, D), BF16),
            dma((4,)), dma((4,)), dma((4,)), dma((2, 8)), dma((2, 8)), dma((2,)), dma((2,)),
        ],
        compiler_params=pltpu.CompilerParams(
            collective_id=0, has_side_effects=True, vmem_limit_bytes=62 * 1024 * 1024
        ),
        name="encoder_processor",
    )(
        grid_send, g2m_sender, mesh_adjacent_lists, mesh_far, mesh_sender,
        g2m_receiver.reshape(1, EDGES), g2m_geom, mesh_geom, mesh_receiver.reshape(1, EDGES),
        mesh_edge_geom, mesh_in, geo_in,
        grid_feat, embed_in, pair_in, square_out,
    )


def solution(mesh):
    split = ("lat", "lon")
    in_specs = (
        P(split, None), P(split, None, None), P(split), P(split), P(None, split), P(None, split),
        P(split, None, None), P(split, None, None), P(split), P(split), P(None, split),
        P(), P(), P(), P(), P(),
    )
    return jax.shard_map(
        per_device, mesh=mesh, in_specs=in_specs, out_specs=P(split, None), check_vma=False
    )
```

time: 331 us -> 112 us (0.34)
  the two profiles are of different devices: /device:TPU:6 before, /device:TPU:1 now
where the time goes in v1:
time: 112 us
  Pallas kernels  107 us (96%)
  local copies, waits for them, and re-layouts  5.41 us (5%)
    pallas_call x1, Pallas kernels, per_device(): pl.pallas_call(kernel, out_shape=jax.ShapeDtypeStruct((NODES, D), BF16),...  107 us
    unnamed x3, local copies, waits for them, and re-layouts  5.41 us

profile of v1, /device:TPU:1, one launch (start us, length us, event | category | flops | bytes accessed | tf_op | source)
XLA Modules:
  0.0 112.0 jit_solution(9722103447671372809)
XLA Ops:
  0.0 1.4 %copy.17.far_lists = s32[1,128,4]{2,1,0:T(8,128)} copy(s32[1,128,4]{1,2,0:T(4,128)} %param.23) | data formatting | bytes 4096 | tf_op args[7]
  1.4 2.3 %copy.18.grid_hbm = bf16[1024,474]{1,0:T(8,128)(2,1)} copy(bf16[1024,474]{0,1:T(8,128)(2,1)} %param.16) | data formatting | bytes 1941504 | tf_op args[0]
  3.7 106.6 %encoder_processor.1 = bf16[320,512]{1,0:T(8,128)(2,1)} custom-call(s32[1,4,256]{2,1,0:T(4,128)} %grid_send.1, s32[4096]{0:T(1024)} %g2m_sender.1, s32[1,8,112]{2,1,0:T(8,128)} %near_lists.1, s32[1,128,4]{2,1,0:T(8,128)} %copy.17.far_lists, s32[4096]{0:T(1024)} %mesh_sender.1, s32[1,4096]{1,0:T(1,128)} %bitcast.2, f32[4,4096]{1,0:T(4,128)} %g2m_geom.1, ...), custom_call_target="tpu_custom_call" | custom-call | tf_op jit(solution)/shard_map/encoder_processor/pallas_call | solution.py:316
  110.3 1.7 %copy.20 = bf16[320,512]{1,0:T(8,128)(2,1)} copy(bf16[320,512]{1,0:T(8,128)(2,1)} %encoder_processor.1) | data formatting | bytes 655360

commit v2 on v1

--- a/solution.py
+++ b/solution.py
@@ -21,6 +21,8 @@
 FAR = 4
 EDGES = 4096
 CHUNK = 512
+HALF = CHUNK // 2
+SLICE = 64
 KX = NODES + 16
 NEAR_ROWS = 8 * NEAR
 MESH_AXES = pl.DeviceIdType.MESH
@@ -31,9 +33,12 @@
     return jnp.dot(left, right, preferred_element_type=F32)
 
 
+def silu_of_half(half):
+    return half * jnp.tanh(half) + half
+
+
 def silu(x):
-    half = 0.5 * x
-    return half * jnp.tanh(half) + half
+    return silu_of_half(0.5 * x)
 
 
 def layer_norm(values):
@@ -69,33 +74,38 @@
     out,
     grid, embed, pair, square,
     table, staged, grid_out, grid_arrived, near_out, near_arrived, far_out, far_arrived,
-    geo_x, geo_w, x_grid, x_mesh, y_rows, pre, gathered, hidden, edge_sum, latent,
+    geo_x, geo_w, x_grid, x_mesh, y_rows, pre, gathered_0, gathered_1, hidden_0, hidden_1, product_0, product_1, message_0, message_1,
+    edge_sum, latent,
     load_sem, grid_ssem, grid_rsem, near_ssem, near_rsem, far_ssem, far_rsem,
 ):
     lat = lax.axis_index("lat")
     lon = lax.axis_index("lon")
     me = lat * N_LON + lon
+    lats = [lax.rem(lat + step, N_LAT) for step in range(N_LAT)]
+    lons = [lax.rem(lon + step, N_LON) for step in range(N_LON)]
+    others = [(a, b) for a in range(N_LAT) for b in range(N_LON) if a or b]
+    gathered, hidden = (gathered_0, gathered_1), (hidden_0, hidden_1)
+    product, message = (product_0, product_1), (message_0, message_1)
 
     loads = [
-        pltpu.make_async_copy(grid_hbm, grid, load_sem.at[0]),
-        pltpu.make_async_copy(embed_hbm, embed, load_sem.at[1]),
-        pltpu.make_async_copy(square_hbm, square, load_sem.at[2]),
-        pltpu.make_async_copy(pair_hbm, pair, load_sem.at[3]),
+        pltpu.make_async_copy(source, target, load_sem.at[k])
+        for k, (source, target) in enumerate((
+            (grid_hbm, grid), (embed_hbm, embed),
+            (square_hbm.at[0], square.at[0]), (pair_hbm.at[0, 0], pair.at[0, 0]),
+            (square_hbm.at[pl.ds(1, 7)], square.at[pl.ds(1, 7)]),
+            (pair_hbm.at[0, pl.ds(1, 3)], pair.at[0, pl.ds(1, 3)]),
+            (pair_hbm.at[pl.ds(1, 2)], pair.at[pl.ds(1, 2)]),
+        ))
     ]
     for load in loads:
         load.start()
 
     barrier = pltpu.get_barrier_semaphore()
 
-    def greet(step, carry):
-        other = lax.rem(me + step, DEVICES)
+    for a, b in others:
         pl.semaphore_signal(
-            barrier, inc=1, device_id=(other // N_LON, lax.rem(other, N_LON)),
-            device_id_type=MESH_AXES,
-        )
-        return carry
-
-    lax.fori_loop(1, DEVICES, greet, 0)
+            barrier, inc=1, device_id=(lats[a], lons[b]), device_id_type=MESH_AXES
+        )
 
     def send_to(offset, source, target, ssem, rsem):
         lat_step, lon_step = offset
@@ -111,29 +121,28 @@
         here = lat - offset[0]
         return jnp.logical_and(here >= 0, here < N_LAT)
 
-    for load in loads:
+    for load in loads[:4]:
         load.wait()
     rows_at_once = 256
 
     def embed_rows(block, carry):
         rows = pl.ds(pl.multiple_of(block * rows_at_once, rows_at_once), rows_at_once)
-        first = silu(matmul(grid[rows, :], embed[...])).astype(BF16)
+        first = lax.dot_general(
+            grid[:, rows], embed[...], (((0,), (0,)), ((), ())), preferred_element_type=F32
+        )
+        first = silu(first).astype(BF16)
         grid_latent = layer_norm(matmul(first, square[0])).astype(BF16)
-        store_rows(table, block * rows_at_once, matmul(grid_latent, pair[0, 0]))
+        store_rows(table, block * rows_at_once, 0.5 * matmul(grid_latent, pair[0, 0]))
         return carry
 
     lax.fori_loop(0, GRID_DEV // rows_at_once, embed_rows, 0)
 
-    def pick(list_ref, first_of, count):
-        def some(block, carry):
-            for k in range(16):
-                slot = block * 16 + k
-                row = list_ref(slot)
-                staged[pl.ds(pl.multiple_of((first_of + slot) * PARTS, PARTS), PARTS), :] = table[
-                    pl.ds(row * PARTS, PARTS), :
-                ]
-            return carry
-        lax.fori_loop(0, count // 16, some, 0)
+    def copy_row(target, slot, row):
+        target[pl.ds(slot * PARTS, PARTS), :] = table[pl.ds(row * PARTS, PARTS), :]
+
+    def pick(row_of, first, count):
+        for k in range(count):
+            copy_row(staged, first + k, row_of(k))
 
     def run_if(condition, offset, act):
         if offset[0] == 0:
@@ -169,8 +178,8 @@
         lax.fori_loop(0, EDGES // CHUNK, some, 0)
 
     def pre_activation(section, x_ref):
-        y_rows[0:NODES, :] = matmul(latent[...], pair[section, 1]).astype(BF16)
-        high, low = split_high_low(geo_in[section])
+        y_rows[0:NODES, :] = (0.5 * matmul(latent[...], pair[section, 1])).astype(BF16)
+        high, low = split_high_low(0.5 * geo_in[section])
         geo_w[0:4, :] = high
         geo_w[4:8, :] = high
         geo_w[8:12, :] = low
@@ -186,6 +195,8 @@
 
         lax.fori_loop(0, EDGES // CHUNK, some, 0)
 
+    for load in loads[4:]:
+        load.wait()
     build_x(x_grid, g2m_receiver, g2m_geom)
     high, low = split_high_low(mesh_geom[...])
     geo_x[0:3, 0:NODES] = high
@@ -203,31 +214,49 @@
     )
     latent[...] = layer_norm(matmul(silu(mesh_first).astype(BF16), square[1])).astype(BF16)
     pre_activation(0, x_grid)
-    build_x(x_mesh, mesh_receiver, mesh_edge_geom)
 
     def edges(section, senders, x_ref):
+        chunks = EDGES // CHUNK
         edge_sum[...] = jnp.zeros((NODES, D), F32)
 
-        def some(block, carry):
-            base = block * CHUNK
-            chunk = pl.ds(pl.multiple_of(base, CHUNK), CHUNK)
-
-            def gather(group, inner):
-                for k in range(32):
-                    slot = group * 32 + k
-                    row = senders[base + slot]
-                    gathered[pl.ds(pl.multiple_of(slot * PARTS, PARTS), PARTS), :] = table[
-                        pl.ds(row * PARTS, PARTS), :
-                    ]
-                return inner
-
-            lax.fori_loop(0, CHUNK // 32, gather, 0)
-            hidden[...] = silu(pre[chunk, :] + load_rows(gathered, 0, CHUNK)).astype(BF16)
-            message = layer_norm(matmul(hidden[...], square[2 + 2 * section])).astype(BF16)
-            edge_sum[...] += matmul(x_ref[0:NODES, chunk], message)
-            return carry
-
-        lax.fori_loop(0, EDGES // CHUNK, some, 0)
+        def gather(block, first, count):
+            for slot in range(first, first + count):
+                copy_row(gathered[block % 2], slot, senders[block * CHUNK + slot])
+
+        def hide(block, first):
+            half = pre[pl.ds(block * CHUNK + first, SLICE), :] + load_rows(
+                gathered[block % 2], first, SLICE
+            )
+            hidden[block % 2][first : first + SLICE, :] = silu_of_half(half).astype(BF16)
+
+        def multiply(block, first, count):
+            product[block % 2][first : first + count, :] = matmul(
+                hidden[block % 2][first : first + count, :], square[2 + 2 * section]
+            )
+
+        def normalize(block, first):
+            message[block % 2][first : first + SLICE, :] = layer_norm(
+                product[block % 2][first : first + SLICE, :]
+            ).astype(BF16)
+
+        def add_up(block):
+            edge_sum[...] += matmul(
+                x_ref[0:NODES, block * CHUNK : (block + 1) * CHUNK], message[block % 2][...]
+            )
+
+        gather(0, 0, CHUNK)
+        for block in range(chunks + 1):
+            for first in range(0, CHUNK, SLICE):
+                if block + 1 < chunks:
+                    gather(block + 1, first, SLICE)
+                if block < chunks:
+                    hide(block, first)
+                if block >= 1:
+                    normalize(block - 1, first)
+                if block < chunks and (first + SLICE) % HALF == 0:
+                    multiply(block, first + SLICE - HALF, HALF)
+            if block >= 1:
+                add_up(block - 1)
 
     def node_update(section):
         before = latent[...]
@@ -248,33 +277,35 @@
     far_waits = []
     for section in (1, 2):
         step = section - 1
-        store_rows(table, 0, matmul(latent[...], pair[section, 0]))
-        for d in (0, 1, 2, 5, 6, 7, 3, 4):
+        store_rows(table, 0, 0.5 * matmul(latent[...], pair[section, 0]))
+        def send_far(step=step):
+            for a, b in others:
+                pltpu.make_async_remote_copy(
+                    far_out.at[step, lats[a] * N_LON + lons[b]], far_arrived.at[step, me],
+                    far_ssem.at[step], far_rsem.at[step],
+                    device_id=(lats[a], lons[b]), device_id_type=MESH_AXES,
+                ).start()
+
+        pick(lambda slot: far_lists[0, slot % FAR, slot // FAR], 0, DEVICES * FAR)
+        far_out[step] = staged[0 : DEVICES * FAR * PARTS, :].astype(BF16).reshape(
+            DEVICES, FAR * PARTS, LANES
+        )
+        far_arrived[step, me] = far_out[step, me]
+        order = (0, 1, 2, 5, 6, 7, 3, 4)
+        for n, d in enumerate(order):
+            pick(lambda slot, d=d: near_lists[0, d, slot], n * NEAR, NEAR)
+            near_out[step, d] = staged[n * NEAR * PARTS : (n + 1) * NEAR * PARTS, :].astype(BF16)
+            if n == 0:
+                send_far()
             offset = MESH_OFFSETS[d]
-            pick(lambda slot, d=d: near_lists[0, d, slot], 0, NEAR)
-            near_out[step, d] = staged[0 : NEAR * PARTS, :].astype(BF16)
             copy, exists = send_to(
                 offset, near_out.at[step, d], near_arrived.at[step, d],
                 near_ssem.at[step, d], near_rsem.at[step, d],
             )
             run_if(exists, offset, copy.start)
             all_sends.append((copy, exists, offset))
-        pick(lambda slot: far_lists[0, slot // FAR, lax.rem(slot, FAR)], 0, DEVICES * FAR)
-        far_out[step] = staged[0 : DEVICES * FAR * PARTS, :].astype(BF16).reshape(
-            DEVICES, FAR * PARTS, LANES
-        )
-        far_arrived[step, me] = far_out[step, me]
-
-        def send_far(k, carry, step=step):
-            other = lax.rem(me + k, DEVICES)
-            pltpu.make_async_remote_copy(
-                far_out.at[step, other], far_arrived.at[step, me],
-                far_ssem.at[step], far_rsem.at[step],
-                device_id=(other // N_LON, lax.rem(other, N_LON)), device_id_type=MESH_AXES,
-            ).start()
-            return carry
-
-        lax.fori_loop(1, DEVICES, send_far, 0)
+        if section == 1:
+            build_x(x_mesh, mesh_receiver, mesh_edge_geom)
         pre_activation(section, x_mesh)
 
         for d, offset in enumerate(MESH_OFFSETS):
@@ -319,7 +350,7 @@
         in_specs=[smem] * 5 + [vmem] * 7 + [hbm] * 4,
         out_specs=vmem,
         scratch_shapes=[
-            pltpu.VMEM((GRID_DEV, C_IN), BF16),
+            pltpu.VMEM((C_IN, GRID_DEV), BF16),
             pltpu.VMEM((C_IN, D), BF16),
             pltpu.VMEM((3, 4, D, D), BF16),
             pltpu.VMEM((8, D, D), BF16),
@@ -337,21 +368,23 @@
             pltpu.VMEM((KX, EDGES), BF16),
             pltpu.VMEM((KX, D), BF16),
             pltpu.VMEM((EDGES, D), F32),
-            pltpu.VMEM((CHUNK * PARTS, LANES), F32),
-            pltpu.VMEM((CHUNK, D), BF16),
+            pltpu.VMEM((CHUNK * PARTS, LANES), F32), pltpu.VMEM((CHUNK * PARTS, LANES), F32),
+            pltpu.VMEM((CHUNK, D), BF16), pltpu.VMEM((CHUNK, D), BF16),
+            pltpu.VMEM((CHUNK, D), F32), pltpu.VMEM((CHUNK, D), F32),
+            pltpu.VMEM((CHUNK, D), BF16), pltpu.VMEM((CHUNK, D), BF16),
             pltpu.VMEM((NODES, D), F32),
             pltpu.VMEM((NODES, D), BF16),
-            dma((4,)), dma((4,)), dma((4,)), dma((2, 8)), dma((2, 8)), dma((2,)), dma((2,)),
+            dma((7,)), dma((4,)), dma((4,)), dma((2, 8)), dma((2, 8)), dma((2,)), dma((2,)),
         ],
         compiler_params=pltpu.CompilerParams(
             collective_id=0, has_side_effects=True, vmem_limit_bytes=62 * 1024 * 1024
         ),
         name="encoder_processor",
     )(
-        grid_send, g2m_sender, mesh_adjacent_lists, mesh_far, mesh_sender,
+        grid_send, g2m_sender, mesh_adjacent_lists, jnp.swapaxes(mesh_far, 1, 2), mesh_sender,
         g2m_receiver.reshape(1, EDGES), g2m_geom, mesh_geom, mesh_receiver.reshape(1, EDGES),
         mesh_edge_geom, mesh_in, geo_in,
-        grid_feat, embed_in, pair_in, square_out,
+        grid_feat.T, embed_in, pair_in, square_out,
     )
 
 

time: 112 us -> 80.8 us (0.72)
  the two profiles are of different devices: /device:TPU:1 before, /device:TPU:6 now
where the time goes in v2:
time: 80.8 us; the launch traced here: 80.6 us
  Pallas kernels  78.9 us (98%)
  local copies, waits for them, and re-layouts  1.72 us (2%)
    pallas_call x1, Pallas kernels, per_device(): pl.pallas_call(kernel, out_shape=jax.ShapeDtypeStruct((NODES, D), BF16),...  78.9 us
    unnamed x1, local copies, waits for them, and re-layouts  1.72 us

profile of v2, /device:TPU:6, one launch (start us, length us, event | category | flops | bytes accessed | tf_op | source)
XLA Modules:
  0.0 80.6 jit_solution(11444669882921690570)
XLA Ops:
  0.0 78.9 %encoder_processor.1 = bf16[320,512]{1,0:T(8,128)(2,1)} custom-call(s32[1,4,256]{2,1,0:T(4,128)} %grid_send.1, s32[4096]{0:T(1024)} %g2m_sender.1, s32[1,8,112]{2,1,0:T(8,128)} %near_lists.1, s32[1,4,128]{2,1,0:T(4,128)} %bitcast.7, s32[4096]{0:T(1024)} %mesh_sender.1, s32[1,4096]{1,0:T(1,128)} %bitcast.5, f32[4,4096]{1,0:T(4,128)} %g2m_geom.1, ...), custom_call_target="tpu_custom_call" | custom-call | tf_op jit(solution)/shard_map/encoder_processor/pallas_call | solution.py:347
  78.9 1.7 %copy.18 = bf16[320,512]{1,0:T(8,128)(2,1)} copy(bf16[320,512]{1,0:T(8,128)(2,1)} %encoder_processor.1) | data formatting | bytes 655360

commit v3 on v2

--- a/solution.py
+++ b/solution.py
@@ -22,7 +22,7 @@
 EDGES = 4096
 CHUNK = 512
 HALF = CHUNK // 2
-SLICE = 64
+SLICE = 32
 KX = NODES + 16
 NEAR_ROWS = 8 * NEAR
 MESH_AXES = pl.DeviceIdType.MESH
@@ -68,14 +68,17 @@
 
 
 def kernel(
+    grid_send_hbm, g2m_sender_hbm, near_lists_hbm, far_lists_hbm, mesh_sender_hbm,
+    g2m_receiver_hbm, g2m_geom_hbm, mesh_geom_hbm, mesh_receiver_hbm, mesh_edge_geom_hbm,
+    mesh_in_hbm, geo_in_hbm, grid_hbm, embed_hbm, pair_hbm, square_hbm,
+    out,
     grid_send, g2m_sender, near_lists, far_lists, mesh_sender,
     g2m_receiver, g2m_geom, mesh_geom, mesh_receiver, mesh_edge_geom, mesh_in, geo_in,
-    grid_hbm, embed_hbm, pair_hbm, square_hbm,
-    out,
+    mesh_rows,
     grid, embed, pair, square,
     table, staged, grid_out, grid_arrived, near_out, near_arrived, far_out, far_arrived,
-    geo_x, geo_w, x_grid, x_mesh, y_rows, pre, gathered_0, gathered_1, hidden_0, hidden_1, product_0, product_1, message_0, message_1,
-    edge_sum, latent,
+    geo_x, geo_w, x_grid, x_mesh, y_rows, pre, gathered_0, gathered_1, hidden_0, hidden_1,
+    product_0, product_1, message_0, message_1, edge_sum, latent,
     load_sem, grid_ssem, grid_rsem, near_ssem, near_rsem, far_ssem, far_rsem,
 ):
     lat = lax.axis_index("lat")
@@ -92,9 +95,14 @@
         for k, (source, target) in enumerate((
             (grid_hbm, grid), (embed_hbm, embed),
             (square_hbm.at[0], square.at[0]), (pair_hbm.at[0, 0], pair.at[0, 0]),
+            (grid_send_hbm, grid_send),
             (square_hbm.at[pl.ds(1, 7)], square.at[pl.ds(1, 7)]),
             (pair_hbm.at[0, pl.ds(1, 3)], pair.at[0, pl.ds(1, 3)]),
             (pair_hbm.at[pl.ds(1, 2)], pair.at[pl.ds(1, 2)]),
+            (g2m_sender_hbm, g2m_sender), (near_lists_hbm, near_lists), (far_lists_hbm, far_lists),
+            (mesh_sender_hbm, mesh_sender), (g2m_receiver_hbm, g2m_receiver), (g2m_geom_hbm, g2m_geom),
+            (mesh_geom_hbm, mesh_geom), (mesh_receiver_hbm, mesh_receiver),
+            (mesh_edge_geom_hbm, mesh_edge_geom), (mesh_in_hbm, mesh_in), (geo_in_hbm, geo_in),
         ))
     ]
     for load in loads:
@@ -150,6 +158,7 @@
         else:
             pl.when(condition)(act)
 
+    loads[4].wait()
     pl.semaphore_wait(barrier, DEVICES - 1)
     grid_sends = []
     for d, offset in enumerate(GRID_OFFSETS):
@@ -160,6 +169,15 @@
         )
         run_if(exists, offset, copy.start)
         grid_sends.append((copy, exists, offset))
+
+    def first_rows(rows, senders, at_once):
+        def some(block, carry):
+            for k in range(at_once):
+                slot = block * at_once + k
+                rows[slot] = senders[slot] * PARTS
+            return carry
+
+        lax.fori_loop(0, EDGES // at_once, some, 0)
 
     def build_x(x_ref, receiver, geometry):
         high, low = split_high_low(geometry[...])
@@ -195,7 +213,7 @@
 
         lax.fori_loop(0, EDGES // CHUNK, some, 0)
 
-    for load in loads[4:]:
+    for load in loads[5:]:
         load.wait()
     build_x(x_grid, g2m_receiver, g2m_geom)
     high, low = split_high_low(mesh_geom[...])
@@ -215,13 +233,15 @@
     latent[...] = layer_norm(matmul(silu(mesh_first).astype(BF16), square[1])).astype(BF16)
     pre_activation(0, x_grid)
 
-    def edges(section, senders, x_ref):
+    def edges(section, sender_rows, scale, x_ref):
         chunks = EDGES // CHUNK
         edge_sum[...] = jnp.zeros((NODES, D), F32)
 
         def gather(block, first, count):
             for slot in range(first, first + count):
-                copy_row(gathered[block % 2], slot, senders[block * CHUNK + slot])
+                gathered[block % 2][slot * PARTS : (slot + 1) * PARTS, :] = table[
+                    pl.ds(sender_rows[block * CHUNK + slot] * scale, PARTS), :
+                ]
 
         def hide(block, first):
             half = pre[pl.ds(block * CHUNK + first, SLICE), :] + load_rows(
@@ -270,69 +290,71 @@
         copy = grid_sends[d][0]
         run_if(source_exists(offset), offset, copy.wait_recv)
         table[pl.ds((GRID_DEV + d * GSLOT) * PARTS, GSLOT * PARTS), :] = grid_arrived[d].astype(F32)
-    edges(0, g2m_sender, x_grid)
+    edges(0, g2m_sender, PARTS, x_grid)
     latent[...] = node_update(0)
 
-    all_sends = list(grid_sends)
-    far_waits = []
-    for section in (1, 2):
-        step = section - 1
+    def near_copy(step, d):
+        return send_to(
+            MESH_OFFSETS[d], near_out.at[step, d], near_arrived.at[step, d],
+            near_ssem.at[step, d], near_rsem.at[step, d],
+        )
+
+    def far_wait(step):
+        return pltpu.make_async_remote_copy(
+            far_out.at[step, pl.ds(0, DEVICES - 1)], far_arrived.at[step, pl.ds(0, DEVICES - 1)],
+            far_ssem.at[step], far_rsem.at[step],
+            device_id=(lat, lons[1]), device_id_type=MESH_AXES,
+        )
+
+    def processor_step(step, carry):
+        section = step + 1
         store_rows(table, 0, 0.5 * matmul(latent[...], pair[section, 0]))
-        def send_far(step=step):
-            for a, b in others:
-                pltpu.make_async_remote_copy(
-                    far_out.at[step, lats[a] * N_LON + lons[b]], far_arrived.at[step, me],
-                    far_ssem.at[step], far_rsem.at[step],
-                    device_id=(lats[a], lons[b]), device_id_type=MESH_AXES,
-                ).start()
-
         pick(lambda slot: far_lists[0, slot % FAR, slot // FAR], 0, DEVICES * FAR)
         far_out[step] = staged[0 : DEVICES * FAR * PARTS, :].astype(BF16).reshape(
             DEVICES, FAR * PARTS, LANES
         )
         far_arrived[step, me] = far_out[step, me]
-        order = (0, 1, 2, 5, 6, 7, 3, 4)
-        for n, d in enumerate(order):
+        for n, d in enumerate((0, 1, 2, 5, 6, 7, 3, 4)):
             pick(lambda slot, d=d: near_lists[0, d, slot], n * NEAR, NEAR)
             near_out[step, d] = staged[n * NEAR * PARTS : (n + 1) * NEAR * PARTS, :].astype(BF16)
             if n == 0:
-                send_far()
-            offset = MESH_OFFSETS[d]
-            copy, exists = send_to(
-                offset, near_out.at[step, d], near_arrived.at[step, d],
-                near_ssem.at[step, d], near_rsem.at[step, d],
+                for a, b in others:
+                    pltpu.make_async_remote_copy(
+                        far_out.at[step, lats[a] * N_LON + lons[b]], far_arrived.at[step, me],
+                        far_ssem.at[step], far_rsem.at[step],
+                        device_id=(lats[a], lons[b]), device_id_type=MESH_AXES,
+                    ).start()
+            copy, exists = near_copy(step, d)
+            run_if(exists, MESH_OFFSETS[d], copy.start)
+
+        @pl.when(step == 0)
+        def _():
+            build_x(x_mesh, mesh_receiver, mesh_edge_geom)
+            first_rows(mesh_rows, mesh_sender, 256)
+
+        pre_activation(section, x_mesh)
+        for d, offset in enumerate(MESH_OFFSETS):
+            run_if(source_exists(offset), offset, near_copy(step, d)[0].wait_recv)
+            table[pl.ds((NODES + d * NEAR) * PARTS, NEAR * PARTS), :] = near_arrived[step, d].astype(
+                F32
             )
-            run_if(exists, offset, copy.start)
-            all_sends.append((copy, exists, offset))
-        if section == 1:
-            build_x(x_mesh, mesh_receiver, mesh_edge_geom)
-        pre_activation(section, x_mesh)
-
+        far_wait(step).wait_recv()
+        table[pl.ds((NODES + NEAR_ROWS) * PARTS, DEVICES * FAR * PARTS), :] = far_arrived[
+            step
+        ].astype(F32).reshape(DEVICES * FAR * PARTS, LANES)
+        edges(section, mesh_rows, 1, x_mesh)
+        latent[...] = node_update(section)
+        return carry
+
+    lax.fori_loop(0, 2, processor_step, 0)
+    out[...] = latent[...]
+    for copy, exists, offset in grid_sends:
+        run_if(exists, offset, copy.wait_send)
+    for step in range(2):
         for d, offset in enumerate(MESH_OFFSETS):
-            copy, exists = send_to(
-                offset, near_out.at[step, d], near_arrived.at[step, d],
-                near_ssem.at[step, d], near_rsem.at[step, d],
-            )
-            run_if(source_exists(offset), offset, copy.wait_recv)
-            table[pl.ds((NODES + d * NEAR) * PARTS, NEAR * PARTS), :] = near_arrived[step, d].astype(F32)
-        far_wait = pltpu.make_async_remote_copy(
-            far_out.at[step, pl.ds(0, DEVICES - 1)], far_arrived.at[step, pl.ds(0, DEVICES - 1)],
-            far_ssem.at[step], far_rsem.at[step],
-            device_id=(lat, lax.rem(lon + 1, N_LON)), device_id_type=MESH_AXES,
-        )
-        far_wait.wait_recv()
-        far_waits.append(far_wait)
-        table[pl.ds((NODES + NEAR_ROWS) * PARTS, DEVICES * FAR * PARTS), :] = far_arrived[step].astype(
-            F32
-        ).reshape(DEVICES * FAR * PARTS, LANES)
-        edges(section, mesh_sender, x_mesh)
-        latent[...] = node_update(section)
-
-    out[...] = latent[...]
-    for copy, exists, offset in all_sends:
-        run_if(exists, offset, copy.wait_send)
-    for far_wait in far_waits:
-        far_wait.wait_send()
+            copy, exists = near_copy(step, d)
+            run_if(exists, offset, copy.wait_send)
+        far_wait(step).wait_send()
 
 
 def per_device(
@@ -340,16 +362,22 @@
     mesh_far, mesh_sender, mesh_receiver, mesh_edge_geom, embed_in, mesh_in, geo_in, pair_in,
     square_out,
 ):
-    smem = pl.BlockSpec(memory_space=pltpu.SMEM)
     vmem = pl.BlockSpec(memory_space=pltpu.VMEM)
     hbm = pl.BlockSpec(memory_space=pl.ANY)
     dma = pltpu.SemaphoreType.DMA
     return pl.pallas_call(
         kernel,
         out_shape=jax.ShapeDtypeStruct((NODES, D), BF16),
-        in_specs=[smem] * 5 + [vmem] * 7 + [hbm] * 4,
+        in_specs=[hbm] * 16,
         out_specs=vmem,
         scratch_shapes=[
+            pltpu.SMEM((1, 4, GSLOT), jnp.int32), pltpu.SMEM((EDGES,), jnp.int32),
+            pltpu.SMEM((1, 8, NEAR), jnp.int32), pltpu.SMEM((1, FAR, DEVICES), jnp.int32),
+            pltpu.SMEM((EDGES,), jnp.int32),
+            pltpu.VMEM((1, EDGES), jnp.int32), pltpu.VMEM((4, EDGES), F32),
+            pltpu.VMEM((3, NODES), F32), pltpu.VMEM((1, EDGES), jnp.int32),
+            pltpu.VMEM((4, EDGES), F32), pltpu.VMEM((3, D), F32), pltpu.VMEM((3, 4, D), F32),
+            pltpu.SMEM((EDGES,), jnp.int32),
             pltpu.VMEM((C_IN, GRID_DEV), BF16),
             pltpu.VMEM((C_IN, D), BF16),
             pltpu.VMEM((3, 4, D, D), BF16),
@@ -374,7 +402,7 @@
             pltpu.VMEM((CHUNK, D), BF16), pltpu.VMEM((CHUNK, D), BF16),
             pltpu.VMEM((NODES, D), F32),
             pltpu.VMEM((NODES, D), BF16),
-            dma((7,)), dma((4,)), dma((4,)), dma((2, 8)), dma((2, 8)), dma((2,)), dma((2,)),
+            dma((19,)), dma((4,)), dma((4,)), dma((2, 8)), dma((2, 8)), dma((2,)), dma((2,)),
         ],
         compiler_params=pltpu.CompilerParams(
             collective_id=0, has_side_effects=True, vmem_limit_bytes=62 * 1024 * 1024

time: 80.8 us -> 79 us (0.978)
  Pallas kernels: 78.9 us -> 77.2 us
    pallas_call x1, Pallas kernels: 78.9 us -> 77.2 us  [per_device(): pl.pallas_call(kernel, out_shape=jax.ShapeDtypeStruct((NODES, D), BF16),...]
where the time goes in v3:
time: 79 us; the launch traced here: 78.9 us
  Pallas kernels  77.2 us (98%)
  local copies, waits for them, and re-layouts  1.72 us (2%)
    pallas_call x1, Pallas kernels, per_device(): pl.pallas_call(kernel, out_shape=jax.ShapeDtypeStruct((NODES, D), BF16),...  77.2 us
    unnamed x1, local copies, waits for them, and re-layouts  1.72 us

profile of v3, /device:TPU:6, one launch (start us, length us, event | category | flops | bytes accessed | tf_op | source)
XLA Modules:
  0.0 78.9 jit_solution(9686214529062384881)
XLA Ops:
  0.0 77.2 %encoder_processor.1 = bf16[320,512]{1,0:T(8,128)(2,1)} custom-call(s32[1,4,256]{2,1,0:T(4,128)} %grid_send_hbm.1, s32[4096]{0:T(1024)} %g2m_sender_hbm.1, s32[1,8,112]{2,1,0:T(8,128)} %near_lists_hbm.1, s32[1,4,128]{2,1,0:T(4,128)} %bitcast.7, s32[4096]{0:T(1024)} %mesh_sender_hbm.1, s32[1,4096]{1,0:T(1,128)} %bitcast.5, f32[4,4096]{1,0:T(4,128)} %g2m_geom_hbm.1, ...), custom_call_target="tpu_custom_call" | custom-call | tf_op jit(solution)/shard_map/encoder_processor/pallas_call | solution.py:368
  77.2 1.7 %copy.18 = bf16[320,512]{1,0:T(8,128)(2,1)} copy(bf16[320,512]{1,0:T(8,128)(2,1)} %encoder_processor.1) | data formatting | bytes 655360

commit v4 on v3

--- a/solution.py
+++ b/solution.py
@@ -47,6 +47,11 @@
     return centre * lax.rsqrt(spread + EPSILON)
 
 
+def scale_to_unit(centred):
+    spread = jnp.sum(centred * centred, axis=-1, keepdims=True) * (1.0 / D)
+    return centred * lax.rsqrt(spread + EPSILON)
+
+
 def split_high_low(values):
     high = values.astype(BF16).astype(F32)
     return high, (values - high).astype(BF16).astype(F32)
@@ -215,6 +220,13 @@
 
     for load in loads[5:]:
         load.wait()
+    def centre(section, carry):
+        weight = square[2 + 2 * section].astype(F32)
+        mean = jnp.sum(weight, axis=-1, keepdims=True) * (1.0 / D)
+        square[2 + 2 * section] = (weight - mean).astype(BF16)
+        return carry
+
+    lax.fori_loop(0, 3, centre, 0)
     build_x(x_grid, g2m_receiver, g2m_geom)
     high, low = split_high_low(mesh_geom[...])
     geo_x[0:3, 0:NODES] = high
@@ -255,7 +267,7 @@
             )
 
         def normalize(block, first):
-            message[block % 2][first : first + SLICE, :] = layer_norm(
+            message[block % 2][first : first + SLICE, :] = scale_to_unit(
                 product[block % 2][first : first + SLICE, :]
             ).astype(BF16)
 

time: 79 us -> 77.7 us (0.984)
  Pallas kernels: 77.2 us -> 75.9 us
    pallas_call x1, Pallas kernels: 77.2 us -> 75.9 us  [per_device(): pl.pallas_call(kernel, out_shape=jax.ShapeDtypeStruct((NODES, D), BF16),...]
where the time goes in v4:
time: 77.7 us; the launch traced here: 77.6 us
  Pallas kernels  75.9 us (98%)
  local copies, waits for them, and re-layouts  1.72 us (2%)
    pallas_call x1, Pallas kernels, per_device(): pl.pallas_call(kernel, out_shape=jax.ShapeDtypeStruct((NODES, D), BF16),...  75.9 us
    unnamed x1, local copies, waits for them, and re-layouts  1.72 us

profile of v4, /device:TPU:6, one launch (start us, length us, event | category | flops | bytes accessed | tf_op | source)
XLA Modules:
  0.0 77.6 jit_solution(5257334235356656795)
XLA Ops:
  0.0 75.9 %encoder_processor.1 = bf16[320,512]{1,0:T(8,128)(2,1)} custom-call(s32[1,4,256]{2,1,0:T(4,128)} %grid_send_hbm.1, s32[4096]{0:T(1024)} %g2m_sender_hbm.1, s32[1,8,112]{2,1,0:T(8,128)} %near_lists_hbm.1, s32[1,4,128]{2,1,0:T(4,128)} %bitcast.7, s32[4096]{0:T(1024)} %mesh_sender_hbm.1, s32[1,4096]{1,0:T(1,128)} %bitcast.5, f32[4,4096]{1,0:T(4,128)} %g2m_geom_hbm.1, ...), custom_call_target="tpu_custom_call" | custom-call | tf_op jit(solution)/shard_map/encoder_processor/pallas_call | solution.py:380
  75.9 1.7 %copy.18 = bf16[320,512]{1,0:T(8,128)(2,1)} copy(bf16[320,512]{1,0:T(8,128)(2,1)} %encoder_processor.1) | data formatting | bytes 655360
